TPU v7x, 32 devices: a whole 2x2x4 slice. The times are simulated.
32 devices in a mesh: row: 4 (over y, core), col: 8 (over z, x).
Axes of the slice: x: 2, y: 2, z: 4, core: 2. Of those that a mesh axis runs over, the one named last changes fastest.
Arguments:
- text_features: bfloat16 [5, 1024, 3584], P(None, ('row', 'col')), may hold values from -18 to 18
- vision_features: bfloat16 [6, 1024, 1024], P(None, ('row', 'col')), may hold values from -18 to 18
Outputs:
- stimulus_terms: float32 [1024, 30], P(('row', 'col'))
- cka: float32 [5, 6], replicated
All inputs are finite; a program needn't handle non-finite values.
Results may differ from a plain program's by a relative error of at most 0.0003.
Values may be sent and summed in bfloat16 or wider, within the bound.
No kernel may reach another device: no remote copies, remote signals or barrier semaphores. Data moves between devices by JAX's collectives and lax.ppermute only.
A program may use at most 192 MiB of HBM per device.

v0:
```python
import jax
import jax.numpy as jnp
from jax import lax
from jax.sharding import PartitionSpec as P


def center_with(features, totals, stimuli_count):
    values = features.astype(jnp.float32)
    return (values - totals[:, None, :] / stimuli_count).astype(jnp.bfloat16)


def local(text_features, vision_features):
    text_layers = text_features.shape[0]
    vision_layers = vision_features.shape[0]
    stimuli_count = text_features.shape[1] * lax.axis_size("row") * lax.axis_size("col")
    text_block, vision_block = (
        lax.all_gather(text_features, "col", axis=1, tiled=True),
        lax.all_gather(vision_features, "col", axis=1, tiled=True),
    )
    text_set, vision_set = (
        lax.all_gather(text_features, "row", axis=1, tiled=True),
        lax.all_gather(vision_features, "row", axis=1, tiled=True),
    )
    text_total, vision_total = lax.psum(
        (
            jnp.sum(text_block.astype(jnp.float32), axis=1),
            jnp.sum(vision_block.astype(jnp.float32), axis=1),
        ),
        "row",
    )
    text_block = center_with(text_block, text_total, stimuli_count)
    text_set = center_with(text_set, text_total, stimuli_count)
    vision_block = center_with(vision_block, vision_total, stimuli_count)
    vision_set = center_with(vision_set, vision_total, stimuli_count)
    text_tiles = jnp.einsum(
        "lrd,lcd->lrc", text_block, text_set, preferred_element_type=jnp.float32
    )
    vision_tiles = jnp.einsum(
        "lrd,lcd->lrc", vision_block, vision_set, preferred_element_type=jnp.float32
    )
    row_share = jnp.einsum(
        "arc,brc->rab", text_tiles, vision_tiles, precision=lax.Precision.HIGHEST
    )
    block_rows = row_share.shape[0]
    cross_part = jnp.sum(row_share, axis=0)
    text_part = jnp.sum(text_tiles * text_tiles, axis=(1, 2))
    vision_part = jnp.sum(vision_tiles * vision_tiles, axis=(1, 2))
    cross, text_self, vision_self = lax.psum((cross_part, text_part, vision_part), ("row", "col"))
    own_share = lax.psum_scatter(
        row_share.reshape(block_rows, text_layers * vision_layers),
        "col",
        scatter_dimension=0,
        tiled=True,
    )
    scale = 1.0 / jnp.sqrt(text_self[:, None] * vision_self[None, :])
    stimulus_terms = own_share * (scale.reshape(1, text_layers * vision_layers) * stimuli_count)
    return (stimulus_terms, cross * scale)


def solution(mesh):
    in_specs = (P(None, ("row", "col"), None), P(None, ("row", "col"), None))
    out_specs = (P(("row", "col"), None), P())
    return jax.shard_map(local, mesh=mesh, in_specs=in_specs, out_specs=out_specs, check_vma=False)
```

profile of v0, /device:TPU:0, one launch (start us, length us, event | category | flops | bytes accessed | tf_op | source)
XLA Modules:
  0.0 381.2 jit_solution(2243413906863889780)
XLA Ops:
  7.2 0.7 all-gather.5.cloned.1.call-update
  7.9 0.7 all-gather.9.cloned.1.call-update
  8.7 0.7 all-gather.11.cloned.1.call-update
  9.4 137.5 %all-gather.5.cloned.1.call-done = bf16[5,256,3584]{2,1,0:T(8,128)(2,1)} async-done(((bf16[5,32,3584]{2,1,0:T(8,128)(2,1)}), bf16[5,256,3584]{2,1,0:T(8,128)(2,1)}) %all-gather.5.cloned.1.call-update) | async-done | bytes 9175056 | tf_op jit(solution)/shard_map/all_gather | solution.py:17
  147.0 5.5 %convert_reduce_fusion = f32[5,3584]{1,0:T(8,128)} fusion(bf16[5,256,3584]{2,1,0:T(8,128)(2,1)} %all-gather.5.cloned.1.call-done), kind=kLoop, calls=%fused_computation.1 | loop fusion | flops 9157120 | bytes 9246720 | tf_op jit(solution)/shard_map/reduce_sum | solution.py:26
  152.6 0.5 all-gather.7.cloned.1.call-update
  153.2 54.2 %all-gather.9.cloned.1.call-done = bf16[6,256,1024]{2,1,0:T(8,128)(2,1)} async-done(((bf16[6,32,1024]{2,1,0:T(8,128)(2,1)}), bf16[6,256,1024]{2,1,0:T(8,128)(2,1)}) %all-gather.9.cloned.1.call-update) | async-done | bytes 3145744 | tf_op jit(solution)/shard_map/all_gather | solution.py:18
  207.4 2.5 convert_reduce_fusion.1
  209.9 11.1 %psum.36 = f32[6,1024]{1,0:T(8,128)S(1)} all-reduce(f32[6,1024]{1,0:T(8,128)S(1)} %convert_reduce_fusion.1), channel_id=1, replica_groups=mesh['row'=4,'col'=8] {'row'}, use_global_device_ids=true, to_apply=%region_3.0 | all-reduce | flops 6144 | bytes 49152 | tf_op jit(solution)/shard_map/psum | solution.py:24
  221.0 6.5 %all-gather.11.cloned.1.call-done = bf16[6,128,1024]{2,1,0:T(8,128)(2,1)} async-done(((bf16[6,32,1024]{2,1,0:T(8,128)(2,1)}), bf16[6,128,1024]{2,1,0:T(8,128)(2,1)}) %all-gather.11.cloned.1.call-update) | async-done | bytes 1572880 | tf_op jit(solution)/shard_map/all_gather | solution.py:22
  227.5 3.5 multiply_reduce_fusion
  231.0 28.9 %all-reduce.3.cloned.1.call-done = f32[5,3584]{1,0:T(8,128)} async-done(((f32[5,3584]{1,0:T(8,128)}), f32[5,3584]{1,0:T(8,128)}) %all-reduce.3.cloned.1.call-update) | async-done | bytes 71696 | tf_op jit(solution)/shard_map/psum | solution.py:24
  259.9 0.9 broadcast_multiply_fusion
  260.8 38.6 %all-gather.7.cloned.1.call-done = bf16[5,128,3584]{2,1,0:T(8,128)(2,1)} async-done(((bf16[5,32,3584]{2,1,0:T(8,128)(2,1)}), bf16[5,128,3584]{2,1,0:T(8,128)(2,1)}) %all-gather.7.cloned.1.call-update) | async-done | bytes 4587536 | tf_op jit(solution)/shard_map/all_gather | solution.py:21
  299.4 7.6 %multiply_reduce_fusion.1 = (f32[5]{0:T(128)S(1)}, f32[5,256,128]{2,1,0:T(8,128)S(1)}) fusion(bf16[5,128,3584]{2,1,0:T(8,128)(2,1)} %all-gather.7.cloned.1.call-done, f32[5,3584]{1,0:T(8,128)S(1)} %broadcast_multiply_fusion, bf16[5,256,3584]{2,1,0:T(8,128)(2,1)} %all-gather.5.cloned.1.call-done), kind=kOutput, calls=%fused_computation.18 | convolution fusion | flops 1195376640 | bytes 14489620 | tf_op jit(solution)/shard_map/lrd,lcd->lrc/dot_general | solution.py:35
  307.0 2.6 fusion.15
  309.6 0.8 reshape.34
  310.5 39.5 %all-reduce = (f32[6]{0:T(128)S(1)}, f32[5]{0:T(128)S(1)}, f32[5,6]{1,0:T(8,128)S(1)}) all-reduce(f32[6]{0:T(128)S(1)} %get-tuple-element.11, f32[5]{0:T(128)S(1)} %get-tuple-element.13, f32[5,6]{1,0:T(8,128)S(1)} %get-tuple-element.15), channel_id=1, replica_groups=mesh['row'=4,'col'=8] {'row','col'}, use_global_device_ids=true, to_apply=%region_8.0 | all-reduce | flops 41 | bytes 328 | tf_op jit(solution)/shard_map/psum | solution.py:48
  349.9 0.7 fusion.13
  350.6 0.1 mul.53
  350.7 22.1 %reduce-scatter.4.cloned.1.call-done = f32[32,30]{1,0:T(8,128)} async-done(((f32[256,30]{1,0:T(8,128)}), f32[32,30]{1,0:T(8,128)}) %reduce-scatter.4.cloned.1.call-update) | async-done | bytes 3856
  372.8 0.8 copy.15
  373.6 0.1 broadcast_multiply_fusion.2
  373.7 0.7 copy.13
  (9 shorter events, 0.3 us)
Async XLA Ops:
  7.2 139.8 %all-gather.5.cloned.1.call-start = ((), (), s32[]{:S(2)}) async-start(), calls=%async_computation.1 | async-start | bytes 10321920 | tf_op jit(solution)/shard_map/all_gather | solution.py:17
  7.9 199.5 %all-gather.9.cloned.1.call-start = ((), (), s32[]{:S(2)}) async-start(), calls=%async_computation.4 | async-start | bytes 3538944 | tf_op jit(solution)/shard_map/all_gather | solution.py:18
  8.6 218.9 %all-gather.11.cloned.1.call-start = ((), (), s32[]{:S(2)}) async-start(), calls=%async_computation.5 | async-start | bytes 1966080 | tf_op jit(solution)/shard_map/all_gather | solution.py:22
  9.4 250.6 %all-reduce.3.cloned.1.call-start = ((), (), s32[]{:S(2)}) async-start(), calls=%async_computation.2 | async-start | bytes 229376 | tf_op jit(solution)/shard_map/psum | solution.py:24
  152.5 146.9 %all-gather.7.cloned.1.call-start = ((), (), s32[]{:S(2)}) async-start(), calls=%async_computation.3 | async-start | bytes 5734400 | tf_op jit(solution)/shard_map/all_gather | solution.py:21
  153.1 219.7 %reduce-scatter.4.cloned.1.call-start = ((), (), s32[]{:S(2)}) async-start(), calls=%async_computation.6 | async-start | bytes 147456
Sparse Core Ops, SparseCore 0:
  10.2 136.7 all-gather.4
  149.1 58.1 all-gather.8
  208.9 18.5 all-gather.10
  229.7 30.1 all-reduce.2
  261.3 38.0 all-gather.6
  310.6 62.1 reduce-scatter.3
where the time goes:
time: 382 us; the launch traced here: 381 us
  waiting for transfers between devices  291 us (76%)
  blocking collectives  50.6 us (13%)
  between operations  14.1 us (4%)
  matrix products  13.6 us (4%)
  other arithmetic  9.69 us (3%)
    all_gather x1, waiting for transfers between devices, local(): lax.all_gather(text_features, 'col', axis=1, tiled=True)  138 us
    all_gather x1, waiting for transfers between devices, local(): lax.all_gather(vision_features, 'col', axis=1, tiled=True)  54.2 us
    psum x1, blocking collectives, local(): lax.psum((cross_part, text_part, vision_part), ('row', 'col'))  39.5 us
    all_gather x1, waiting for transfers between devices, local(): lax.all_gather(text_features, 'row', axis=1, tiled=True)  38.6 us
    psum x1, waiting for transfers between devices, local(): lax.psum((jnp.sum(text_block.astype(jnp.float32), axis=1), jnp.sum(vision...  28.9 us
    unnamed x7, waiting for transfers between devices  24.8 us
    psum x1, blocking collectives, local(): lax.psum((jnp.sum(text_block.astype(jnp.float32), axis=1), jnp.sum(vision...  11.1 us
  transfers between devices with their start and end apart: 6, of which 6 were waited for; matrix products, arithmetic and copies ran while one was open for 3% of the time, Pallas kernels for 0%

commit v1 on v0

--- a/solution.py
+++ b/solution.py
@@ -18,7 +18,7 @@
         lax.all_gather(vision_features, "col", axis=1, tiled=True),
     )
     text_set, vision_set = (
-        lax.all_gather(text_features, "row", axis=1, tiled=True),
+        jnp.concatenate(lax.all_gather(text_features, axis_name="row"), 1),
         lax.all_gather(vision_features, "row", axis=1, tiled=True),
     )
     text_total, vision_total = lax.psum(

time: 382 us -> 386 us (1.010)
  waiting for transfers between devices: 291 us -> 282 us
  other arithmetic: 9.69 us -> 17.9 us
  local copies, waits for them, and re-layouts: 2.41 us -> 6.58 us
    all_gather x1, waiting for transfers between devices: 54.2 us -> 62.9 us  [local(): lax.all_gather(vision_features, 'col', axis=1, tiled=True)]
    convert_element_type x0 -> x2, other arithmetic: none -> 8.21 us  [the longest x1 4.65 us: center_with(): return (values - totals[:, None, :] / stimuli_count).astype(jnp.bfloat16)]
    all_gather x1, waiting for transfers between devices: 38.6 us -> 30.7 us  [local(): lax.all_gather(text_features, axis_name='row')]
    all_gather x1, waiting for transfers between devices: 138 us -> 133 us  [local(): lax.all_gather(text_features, 'col', axis=1, tiled=True)]
    convert_element_type x0 -> x1, local copies, waits for them, and re-layouts: none -> 4.17 us  [center_with(): values = features.astype(jnp.float32)]
    psum x1, waiting for transfers between devices: 28.9 us -> 24.8 us  [local(): lax.psum((jnp.sum(text_block.astype(jnp.float32), axis=1), jnp.sum(vision...]
  transfers between devices with their start and end apart: 6 -> 6, of which waited for: 6 -> 6; matrix products, arithmetic and copies ran while one was open for 3% -> 5% of each run, Pallas kernels for 0% -> 0%
where the time goes in v1:
time: 386 us; the launch traced here: 385 us
  waiting for transfers between devices  282 us (73%)
  blocking collectives  51.9 us (13%)
  other arithmetic  17.9 us (5%)
  between operations  14.2 us (4%)
  matrix products  12.2 us (3%)
  local copies, waits for them, and re-layouts  6.58 us (2%)
    all_gather x1, waiting for transfers between devices, local(): lax.all_gather(text_features, 'col', axis=1, tiled=True)  133 us
    all_gather x1, waiting for transfers between devices, local(): lax.all_gather(vision_features, 'col', axis=1, tiled=True)  62.9 us
    psum x1, blocking collectives, local(): lax.psum((cross_part, text_part, vision_part), ('row', 'col'))  40.7 us
    all_gather x1, waiting for transfers between devices, local(): lax.all_gather(text_features, axis_name='row')  30.7 us
    unnamed x7, waiting for transfers between devices  24.9 us
    psum x1, waiting for transfers between devices, local(): lax.psum((jnp.sum(text_block.astype(jnp.float32), axis=1), jnp.sum(vision...  24.8 us
    psum x1, blocking collectives, local(): lax.psum((jnp.sum(text_block.astype(jnp.float32), axis=1), jnp.sum(vision...  11.1 us
  transfers between devices with their start and end apart: 6, of which 6 were waited for; matrix products, arithmetic and copies ran while one was open for 5% of the time, Pallas kernels for 0%

profile of v1, /device:TPU:0, one launch (start us, length us, event | category | flops | bytes accessed | tf_op | source)
XLA Modules:
  0.0 385.5 jit_solution(2303872813381417181)
XLA Ops:
  7.2 0.7 all-gather.8.cloned.1.call-update
  7.9 0.7 all-gather.10.cloned.1.call-update
  8.7 0.7 all-gather.6.cloned.1.call-update
  10.0 62.9 %all-gather.8.cloned.1.call-done = bf16[6,256,1024]{2,1,0:T(8,128)(2,1)} async-done(((bf16[6,32,1024]{2,1,0:T(8,128)(2,1)}), bf16[6,256,1024]{2,1,0:T(8,128)(2,1)}) %all-gather.8.cloned.1.call-update) | async-done | bytes 3145744 | tf_op jit(solution)/shard_map/all_gather | solution.py:18
  72.9 2.5 convert_reduce_fusion.1
  75.4 11.1 %psum.36 = f32[6,1024]{1,0:T(8,128)S(1)} all-reduce(f32[6,1024]{1,0:T(8,128)S(1)} %convert_reduce_fusion.1), channel_id=1, replica_groups=mesh['row'=4,'col'=8] {'row'}, use_global_device_ids=true, to_apply=%region_3.0 | all-reduce | flops 6144 | bytes 49152 | tf_op jit(solution)/shard_map/psum | solution.py:24
  86.6 6.5 %all-gather.10.cloned.1.call-done = bf16[6,128,1024]{2,1,0:T(8,128)(2,1)} async-done(((bf16[6,32,1024]{2,1,0:T(8,128)(2,1)}), bf16[6,128,1024]{2,1,0:T(8,128)(2,1)}) %all-gather.10.cloned.1.call-update) | async-done | bytes 1572880 | tf_op jit(solution)/shard_map/all_gather | solution.py:22
  93.1 3.4 multiply_reduce_fusion
  96.5 132.7 %all-gather.6.cloned.1.call-done = bf16[5,256,3584]{2,1,0:T(8,128)(2,1)} async-done(((bf16[5,32,3584]{2,1,0:T(8,128)(2,1)}), bf16[5,256,3584]{2,1,0:T(8,128)(2,1)}) %all-gather.6.cloned.1.call-update) | async-done | bytes 9175056 | tf_op jit(solution)/shard_map/all_gather | solution.py:17
  229.2 5.6 %convert_reduce_fusion = f32[5,3584]{1,0:T(8,128)} fusion(bf16[5,256,3584]{2,1,0:T(8,128)(2,1)} %all-gather.6.cloned.1.call-done), kind=kLoop, calls=%fused_computation.1 | loop fusion | flops 9157120 | bytes 9246720 | tf_op jit(solution)/shard_map/reduce_sum | solution.py:26
  234.8 30.7 %all-gather.12.cloned.1.call-done = bf16[20,32,3584]{2,1,0:T(8,128)(2,1)} async-done(((bf16[5,32,3584]{2,1,0:T(8,128)(2,1)}), bf16[20,32,3584]{2,1,0:T(8,128)(2,1)}) %all-gather.12.cloned.1.call-update) | async-done | bytes 4587536 | tf_op jit(solution)/shard_map/all_gather | solution.py:21
  265.5 3.6 convert_bitcast_fusion
  269.1 4.2 %copy.12 = f32[5,4,32,3584]{3,2,1,0:T(8,128)} copy(f32[5,4,32,3584]{3,2,0,1:T(8,128)S(1)} %convert_bitcast_fusion) | data formatting | bytes 18350080 | tf_op jit(solution)/shard_map/convert_element_type | solution.py:8
  273.2 24.8 %all-reduce.3.cloned.1.call-done = f32[5,3584]{1,0:T(8,128)} async-done(((f32[5,3584]{1,0:T(8,128)}), f32[5,3584]{1,0:T(8,128)}) %all-reduce.3.cloned.1.call-update) | async-done | bytes 71696 | tf_op jit(solution)/shard_map/psum | solution.py:24
  298.1 0.9 broadcast_multiply_fusion
  299.0 4.7 %fusion.3 = bf16[5,128,3584]{2,1,0:T(8,128)(2,1)S(1)} fusion(f32[5,4,32,3584]{3,2,1,0:T(8,128)} %copy.12, f32[5,3584]{1,0:T(8,128)S(1)} %broadcast_multiply_fusion), kind=kLoop, calls=%fused_computation.6 | loop fusion | flops 4587520 | bytes 13834240 | tf_op jit(solution)/shard_map/convert_element_type | solution.py:9
  303.6 6.2 %multiply_reduce_fusion.1 = (f32[5]{0:T(128)S(1)}, f32[5,256,128]{2,1,0:T(8,128)S(1)}) fusion(bf16[5,128,3584]{2,1,0:T(8,128)(2,1)S(1)} %fusion.3, bf16[5,256,3584]{2,1,0:T(8,128)(2,1)} %all-gather.6.cloned.1.call-done, f32[5,3584]{1,0:T(8,128)S(1)} %broadcast_multiply_fusion), kind=kOutput, calls=%fused_computation.19 | convolution fusion | flops 1188495360 | bytes 14489620 | tf_op jit(solution)/shard_map/lrd,lcd->lrc/dot_general | solution.py:35
  309.9 2.6 fusion.15
  312.4 0.8 reshape.41
  313.3 40.7 %all-reduce = (f32[6]{0:T(128)S(1)}, f32[5]{0:T(128)S(1)}, f32[5,6]{1,0:T(8,128)S(1)}) all-reduce(f32[6]{0:T(128)S(1)} %get-tuple-element.11, f32[5]{0:T(128)S(1)} %get-tuple-element.13, f32[5,6]{1,0:T(8,128)S(1)} %get-tuple-element.15), channel_id=1, replica_groups=mesh['row'=4,'col'=8] {'row','col'}, use_global_device_ids=true, to_apply=%region_8.0 | all-reduce | flops 41 | bytes 328 | tf_op jit(solution)/shard_map/psum | solution.py:48
  354.0 0.7 fusion.13
  354.8 22.3 %reduce-scatter.4.cloned.1.call-done = f32[32,30]{1,0:T(8,128)} async-done(((f32[256,30]{1,0:T(8,128)}), f32[32,30]{1,0:T(8,128)}) %reduce-scatter.4.cloned.1.call-update) | async-done | bytes 3856
  377.1 0.8 copy.18
  377.9 0.7 copy.16
  (12 shorter events, 0.9 us)
Async XLA Ops:
  7.2 65.8 %all-gather.8.cloned.1.call-start = ((), (), s32[]{:S(2)}) async-start(), calls=%async_computation.3 | async-start | bytes 3538944 | tf_op jit(solution)/shard_map/all_gather | solution.py:18
  7.9 85.2 %all-gather.10.cloned.1.call-start = ((), (), s32[]{:S(2)}) async-start(), calls=%async_computation.4 | async-start | bytes 1966080 | tf_op jit(solution)/shard_map/all_gather | solution.py:22
  8.6 220.5 %all-gather.6.cloned.1.call-start = ((), (), s32[]{:S(2)}) async-start(), calls=%async_computation.1 | async-start | bytes 10321920 | tf_op jit(solution)/shard_map/all_gather | solution.py:17
  9.4 256.1 %all-gather.12.cloned.1.call-start = ((), (), s32[]{:S(2)}) async-start(), calls=%async_computation.5 | async-start | bytes 5734400 | tf_op jit(solution)/shard_map/all_gather | solution.py:21
  10.0 288.1 %all-reduce.3.cloned.1.call-start = ((), (), s32[]{:S(2)}) async-start(), calls=%async_computation.2 | async-start | bytes 229376 | tf_op jit(solution)/shard_map/psum | solution.py:24
  234.8 142.3 %reduce-scatter.4.cloned.1.call-start = ((), (), s32[]{:S(2)}) async-start(), calls=%async_computation.6 | async-start | bytes 147456
Sparse Core Ops, SparseCore 0:
  10.2 62.7 all-gather.7
  74.5 18.5 all-gather.9
  95.3 133.8 all-gather.5
  230.6 34.8 all-gather.11
  267.7 30.3 all-reduce.2
  313.4 63.5 reduce-scatter.3
